TPU v7x, 32 devices: a whole 2x2x4 slice. The times are simulated.
32 devices in a mesh: user: 8 (over z, x), pos: 4 (over y, core).
Axes of the slice: x: 2, y: 2, z: 4, core: 2. Of those that a mesh axis runs over, the one named last changes fastest.
Arguments:
- events: bfloat16 [8192, 256], P('user'), may hold values from -6 to 6
- owners: int32 [8192], P('user'), may hold values from 0 to 15, as said below
- offsets: int32 [8192], P('user'), may hold values from 0 to 2047, as said below
- w_key: bfloat16 [256, 256], replicated, may hold values from -0.375 to 0.375
- w_value: bfloat16 [256, 256], replicated, may hold values from -0.375 to 0.375
- cache_keys: bfloat16 [16, 6144, 256], P('user', 'pos'), may hold values from -7 to 7
- cache_values: bfloat16 [16, 6144, 256], P('user', 'pos'), may hold values from -6 to 6
- hist_len: int32 [16], P('user'), may hold values from 8 to 4096
- active: int32 [16], P('user'), may hold values 0 or 1
- candidates: bfloat16 [16, 1024, 256], P('user', 'pos'), may hold values from -100 to 100
Outputs:
- new_keys: bfloat16 [16, 6144, 256], P('user', 'pos')
- new_values: bfloat16 [16, 6144, 256], P('user', 'pos')
- attended: bfloat16 [16, 1024, 256], P('user', 'pos')
Inputs may be any that keep to these rules, and one draw needn't show every extreme that they name: Among the events of one aligned block of 1024 (one index of user), at most 256 have owners among the users t * 2 to t * 2 + 1, for every t; in every draw some t receives exactly 256 from every block, and all those events belong to one user of that t. offsets[e] is the number of events before e, in the order of the array, that have the same owner as e.
All inputs are finite; a program needn't handle non-finite values. No bound on the sum of `active` on one device may be relied on, other than what follows from the above.
Results may differ from a plain program's by a relative error of at most 0.0067.
Values may be sent and summed in bfloat16 or wider, within the bound.
A program may use at most 128 MiB of HBM per device.

v0:
```python
import functools
import math

import jax
import jax.numpy as jnp
from jax import lax
from jax.experimental import pallas as pl
from jax.experimental.pallas import tpu as pltpu
from jax.sharding import PartitionSpec as P

MESH = pl.DeviceIdType.MESH
NT = (((1,), (1,)), ((), ()))
TAIL = 16
STEP = 64


def pos_peers():
    p = lax.axis_index("pos")
    near = p + 1 - 2 * lax.rem(p, 2)
    far = lax.rem(p + 2, 4)
    return p, near, far


def merged_kernel(
    groups, users_here, cap, scale,
    owners_ref, hist_ref, active_ref, events_hbm, cand_hbm, keys_hbm, values_hbm,
    w_key_hbm, w_value_hbm,
    fresh_ref, counts_ref, out_ref, keys_ref, values_ref,
    events_ref, queries, weight_ref, rows_ref, packed, flipped, eye,
    acc, stat, near_out, near_part, near_stat, far_out, far_stat_out, far_part, far_stat,
    load_sem, a2a_send, a2a_recv, hop_send, hop_recv, q_send, q_recv,
    near_send, near_recv, far_send, far_recv,
):
    me = lax.axis_index("user")
    p, near, far = pos_peers()
    low, high = lax.rem(p, 2), p // 2
    cross = 2 * (1 - high) + 1 - low
    half = groups // 2

    def partner(k, odd):
        bit = lax.rem(me, 2)
        there = me + odd * (1 - 2 * bit)
        for n in range(1, groups.bit_length() - 1):
            if (2 * k >> n) % 2:
                there += (1 - 2 * lax.rem(me // 2**n, 2)) * 2**n
        return there

    peers = [partner(k, low) for k in range(half)]
    near_sources = [partner(k, 1 - low) for k in range(half)]
    sends = list(range(half))[::-1]
    block_rows, width = keys_ref.shape[1:]
    quarter = queries.shape[2]

    def load(src, dst, n):
        copy = pltpu.make_async_copy(src, dst, load_sem.at[n])
        copy.start()
        return copy

    events_in = load(events_hbm, events_ref, 0)
    own_q = load(cand_hbm, queries.at[p], 1)
    keys_in = load(keys_hbm, keys_ref, 2)
    values_in = load(values_hbm, values_ref, 3)
    weights_in = [load(w_key_hbm, weight_ref.at[0], 4), load(w_value_hbm, weight_ref.at[1], 5)]

    barrier = pltpu.get_barrier_semaphore()
    for peer in (near, far):
        pl.semaphore_signal(barrier, inc=1, device_id={"pos": peer}, device_id_type=MESH)
    for peer in peers:
        @pl.when(peer != me)
        def _():
            pl.semaphore_signal(barrier, inc=1, device_id={"user": peer}, device_id_type=MESH)

    per_event = events_ref.shape[0]
    features = events_ref.shape[1]
    users = groups * users_here
    owner = owners_ref[...]
    user_id = lax.broadcasted_iota(jnp.int32, (users, per_event), 0)
    same = (user_id == owner).astype(jnp.float32)
    before = (
        lax.broadcasted_iota(jnp.int32, (per_event, per_event), 0)
        <= lax.broadcasted_iota(jnp.int32, (per_event, per_event), 1)
    ).astype(jnp.float32).astype(jnp.bfloat16)
    ranks = jnp.dot(same.astype(jnp.bfloat16), before, preferred_element_type=jnp.float32)
    counts = jnp.sum(same, axis=1, keepdims=True)
    dest = owner // users_here
    earlier = (user_id >= dest * users_here) & (user_id < owner)
    slot = jnp.sum(jnp.where(earlier, counts, 0.0) + same * ranks, axis=0, keepdims=True) - 1.0
    slot = slot.astype(jnp.int32)
    slot_id = lax.broadcasted_iota(jnp.int32, (cap, per_event), 0)
    lane = lax.broadcasted_iota(jnp.int32, (users, features), 1)
    lane_user = lax.broadcasted_iota(jnp.int32, (users, features), 0)

    def hop(ref_src, ref_dst, send, recv, peer):
        return pltpu.make_async_remote_copy(
            src_ref=ref_src, dst_ref=ref_dst, send_sem=send, recv_sem=recv,
            device_id={"pos": peer}, device_id_type=MESH,
        )

    def q_hop(n, c, u, peer):
        return hop(queries.at[c, u], queries.at[c, u], q_send.at[n, u], q_recv.at[n, u], peer)

    def a2a(k):
        return pltpu.make_async_remote_copy(
            src_ref=packed.at[k], dst_ref=rows_ref.at[me],
            send_sem=a2a_send.at[k], recv_sem=a2a_recv.at[k],
            device_id={"user": peers[k]}, device_id_type=MESH,
        )

    def own(k):
        return pltpu.make_async_copy(packed.at[k], rows_ref.at[me], load_sem.at[6])

    def pack(k):
        peer = peers[k]
        wanted = jnp.where(dest == peer, slot, -1)
        pick = (wanted == slot_id).astype(jnp.float32).astype(jnp.bfloat16)
        packed[k, :cap, :] = jnp.dot(
            pick, events_ref[...], preferred_element_type=jnp.float32
        ).astype(jnp.bfloat16)
        row = jnp.sum(
            jnp.where(lane_user == lane + peer * users_here, counts, 0.0), axis=0, keepdims=True
        )
        packed[k, cap:, :] = jnp.broadcast_to(row, (TAIL, features)).astype(jnp.bfloat16)

    def post(k):
        @pl.when(peers[k] != me)
        def _():
            a2a(k).start()

        if k == 0:
            @pl.when(peers[k] == me)
            def _():
                own(k).start()

    def arrive(k):
        @pl.when(peers[k] != me)
        def _():
            a2a(k).wait_recv()

        if k == 0:
            @pl.when(peers[k] == me)
            def _():
                own(k).wait()

        forward(k, peers[k]).start()

    def forward(k, source):
        block = rows_ref.at[source]
        return hop(block, block, hop_send.at[k], hop_recv.at[k], near)

    events_in.wait()
    early = half // 2
    for k in sends[:early]:
        pack(k)
    own_q.wait()
    pl.semaphore_wait(barrier, 1 + half + low)
    for u in range(users_here):
        q_hop(0, p, u, far).start()
    for u in range(users_here):
        q_hop(1, p, u, near).start()
    for k in sends[:early]:
        post(k)
    for k in sends[early:]:
        pack(k)
        post(k)

    eye[...] = (
        lax.broadcasted_iota(jnp.int32, (width, width), 0)
        == lax.broadcasted_iota(jnp.int32, (width, width), 1)
    ).astype(jnp.float32).astype(jnp.bfloat16)
    factor = scale * math.log2(math.e)
    position = lax.broadcasted_iota(jnp.int32, (block_rows, quarter), 0) + p * block_rows
    keys_in.wait()
    values_in.wait()

    def flip(rows):
        return lax.dot_general(
            eye[...], rows, NT, preferred_element_type=jnp.float32
        ).astype(jnp.bfloat16)

    for u in range(users_here):
        flipped[u] = flip(values_ref[u])

    def two_rows(top, total):
        return jnp.concatenate(
            [jnp.broadcast_to(top, (4, quarter)), jnp.broadcast_to(total, (4, quarter))], axis=0
        )

    def weigh(scores, floor):
        top = jnp.maximum(jnp.max(scores, axis=0, keepdims=True) * factor, floor)
        expo = jnp.exp2(scores * factor - top)
        return top, jnp.sum(expo, axis=0, keepdims=True), expo.astype(jnp.bfloat16)

    def copies(pairs, send, recv, n, peer):
        return [
            hop(src, dst, send.at[i, n], recv.at[i, n], peer)
            for i, (src, dst) in enumerate(pairs)
        ]

    def near_copies(n, u):
        return copies(
            (
                (near_out.at[n, u], near_part.at[n, u]),
                (stat.at[2 + n, u], near_stat.at[n, u]),
            ),
            near_send, near_recv, n * users_here + u, near,
        )

    def far_copies(u):
        return copies(
            ((far_out.at[u], far_part.at[u]), (far_stat_out.at[u], far_stat.at[u])),
            far_send, far_recv, u, far,
        )

    def merge(top, total, part, other, other_part):
        new_top = jnp.maximum(top, other[0:1])
        mine = jnp.exp2(top - new_top)
        theirs = jnp.exp2(other[0:1] - new_top)
        total = total * mine + other[4:5] * theirs
        return new_top, total, part * mine + other_part.astype(jnp.float32) * theirs

    def send_far(u):
        for copy in near_copies(1, u):
            copy.wait_recv()
        old = stat[1, u]
        top, total, part = merge(
            old[0:1], old[4:5], acc[1, u], near_stat[1, u], near_part[1, u]
        )
        far_out[u] = part.astype(jnp.bfloat16)
        far_stat_out[u] = two_rows(top, total)
        for copy in far_copies(u):
            copy.start()

    chunk = (p, far, near, cross)

    def ready(kind, u):
        if kind == 2:
            q_hop(1, near, u, near).wait_recv()
        if kind == 1:
            q_hop(0, far, u, far).wait_recv()
            q_hop(2, far, u, near).start()
        if kind == 3:
            q_hop(2, cross, u, near).wait_recv()

    def finish(kind, u, scores):
        top, total, weights = weigh(jnp.where(position < hist_ref[u], scores, -1e33), -1e29)
        part = jnp.dot(flipped[u], weights, preferred_element_type=jnp.float32)
        stat[kind, u] = two_rows(top, total)
        if kind < 2:
            acc[kind, u] = part
        else:
            near_out[kind - 2, u] = part.astype(jnp.bfloat16)
            for copy in near_copies(kind - 2, u):
                copy.start()
        if kind == 1 and u > 0:
            send_far(u - 1)

    items = [(0, u) for u in range(users_here)]
    for u in range(users_here):
        items += [(2, u), (1, u), (3, u)]
    last = None
    for kind, u in items:
        ready(kind, u)
        scores = lax.dot_general(
            keys_ref[u], queries[chunk[kind], u], NT, preferred_element_type=jnp.float32
        )
        if last is not None:
            finish(*last)
        last = (kind, u, scores)
    finish(*last)
    send_far(users_here - 1)
    for u in range(users_here):
        for copy in near_copies(0, u):
            copy.wait_recv()
        old = stat[0, u]
        top, total, part = merge(
            old[0:1], old[4:5], acc[0, u], near_stat[0, u], near_part[0, u]
        )
        acc[0, u] = part
        stat[0, u] = two_rows(top, total)
    for copy in weights_in:
        copy.wait()

    slots = lax.broadcasted_iota(jnp.int32, (cap, quarter), 0).astype(jnp.float32)

    def project(source):
        raw = rows_ref[source, :cap, :]
        row = pl.multiple_of(STEP + source * cap, 8)
        made = []
        for i in range(2):
            product = jnp.dot(raw, weight_ref[i], preferred_element_type=jnp.float32)
            product = product.astype(jnp.bfloat16)
            made.append(product)
            for n in range(width // 128):
                fresh_ref[i * (width // 128) + n, pl.ds(row, cap)] = product[
                    :, n * 128 : n * 128 + 128
                ].astype(jnp.float32)
        tail = rows_ref[source, cap:, :].astype(jnp.float32)
        begin = jnp.zeros((1, 1), jnp.float32)
        mask = []
        for u in range(users_here):
            end = begin + tail[0:1, u : u + 1]
            mask.append((slots >= begin) & (slots < end))
            begin = end
        return made[0], flip(made[1]), mask

    def fresh(sources):
        blocks = [project(source) for source in sources]
        keys_new = jnp.concatenate([b[0] for b in blocks], axis=0)
        flipped_new = jnp.concatenate([b[1] for b in blocks], axis=1)
        scores = [
            lax.dot_general(keys_new, queries[p, u], NT, preferred_element_type=jnp.float32)
            for u in range(users_here)
        ]
        for u in range(users_here):
            mask = jnp.concatenate([b[2][u] for b in blocks], axis=0)
            old = stat[0, u]
            top, total, weights = weigh(jnp.where(mask, scores[u], -1e33), old[0:1])
            shrink = jnp.exp2(old[0:1] - top)
            acc[0, u] = acc[0, u] * shrink + jnp.dot(
                flipped_new, weights, preferred_element_type=jnp.float32
            )
            stat[0, u] = two_rows(top, total + old[4:5] * shrink)

    soon = range(half // 2)
    late = range(half // 2, half)
    for k in soon:
        arrive(k)
    for k in soon:
        forward(k, near_sources[k]).wait_recv()
    fresh([source for k in soon for source in (peers[k], near_sources[k])])
    for k in late:
        arrive(k)
    fresh([peers[k] for k in late])
    for k in late:
        forward(k, near_sources[k]).wait_recv()
    fresh([near_sources[k] for k in late])
    for g in range(groups):
        counts_ref[g : g + 1, :] = rows_ref[g, cap : cap + TAIL, :128].astype(jnp.float32)[
            0:1
        ].astype(jnp.int32)

    for u in range(users_here):
        for copy in far_copies(u):
            copy.wait_recv()
        mine = stat[0, u]
        top, total, part = merge(mine[0:1], mine[4:5], acc[0, u], far_stat[u], far_part[u])
        flag = active_ref[u].astype(jnp.float32)
        out_ref[u] = (part * (flag / total)).T.astype(jnp.bfloat16)
    for u in range(users_here):
        q_hop(0, p, u, far).wait_send()
        q_hop(1, p, u, near).wait_send()
        q_hop(2, far, u, near).wait_send()
        for n in range(2):
            for copy in near_copies(n, u):
                copy.wait_send()
        for copy in far_copies(u):
            copy.wait_send()
    for k in range(half):
        @pl.when(peers[k] != me)
        def _():
            a2a(k).wait_send()

        forward(k, peers[k]).wait_send()


def place_kernel(
    groups, cap,
    count_ref, hist_ref, made_ref, keys_ref, values_ref, attended_ref,
    new_keys_hbm, new_values_hbm, out_hbm,
    cache, out_sem, read_sem,
):
    users_here, rows, width = keys_ref.shape
    sources = (keys_ref, values_ref)
    targets = (new_keys_hbm, new_values_hbm)
    origin = lax.axis_index("pos") * rows
    read = pltpu.make_async_copy(attended_ref, out_hbm, read_sem)
    read.start()

    def leave(u, i, source):
        return pltpu.make_async_copy(source, targets[i].at[u], out_sem.at[u, i])

    begin = [hist_ref[u] - origin for u in range(users_here)]
    end = [
        lax.fori_loop(0, groups, lambda g, n, u=u: n + count_ref[g, u], begin[u])
        for u in range(users_here)
    ]
    touched = [
        (begin[u] < rows) & (end[u] > 0) & (end[u] > begin[u]) for u in range(users_here)
    ]
    for u in range(users_here):
        @pl.when(jnp.logical_not(touched[u]))
        def _():
            for i in range(2):
                leave(u, i, sources[i].at[u]).start()

    row = lax.broadcasted_iota(jnp.int32, (STEP, 128), 0)
    for u in range(users_here):
        @pl.when(touched[u])
        def _():
            for i in range(2):
                cache[u, i] = sources[i][u]

            def place(g, at):
                size = count_ref[g, u]

                @pl.when((size > 0) & (at < rows) & (at + size > 0))
                def _():
                    low = lax.fori_loop(0, u, lambda v, n: n + count_ref[g, v], 0)
                    first = jnp.maximum(at, 0) // 16 * 16
                    last = jnp.minimum(at + size, rows)

                    def blend(n, carry):
                        to = pl.multiple_of(jnp.minimum(first + n * STEP, rows - STEP), 16)
                        start = STEP + g * cap + low + to - at
                        inside = (row >= at - to) & (row < at + size - to)
                        for i in range(2):
                            for tile in range(width // 128):
                                lanes = slice(tile * 128, tile * 128 + 128)
                                fresh = made_ref[i * (width // 128) + tile, pl.ds(start, STEP), :]
                                old = cache[u, i, pl.ds(to, STEP), lanes].astype(jnp.float32)
                                cache[u, i, pl.ds(to, STEP), lanes] = jnp.where(
                                    inside, fresh, old
                                ).astype(jnp.bfloat16)
                        return carry

                    lax.fori_loop(0, (last - first + STEP - 1) // STEP, blend, 0)

                return at + size

            lax.fori_loop(0, groups, place, begin[u])
            for i in range(2):
                leave(u, i, cache.at[u, i]).start()

    for u in range(users_here):
        for i in range(2):
            leave(u, i, sources[i].at[u]).wait()
    read.wait()


def on_device(
    events, owners, offsets, w_key, w_value, cache_keys, cache_values, hist_len, active, candidates
):
    groups = lax.axis_size("user")
    blocks = lax.axis_size("pos")
    users_here, block_rows, width = cache_keys.shape
    per_event, features = events.shape
    cap = 2 * per_event // groups
    quarter = candidates.shape[1]
    half = groups // 2
    vmem = pl.BlockSpec(memory_space=pltpu.VMEM)
    smem = pl.BlockSpec(memory_space=pltpu.SMEM)
    hbm = pl.BlockSpec(memory_space=pltpu.HBM)
    dma = pltpu.SemaphoreType.DMA
    bf16, f32 = jnp.bfloat16, jnp.float32

    made, counts, attended, keys, values = pl.pallas_call(
        functools.partial(merged_kernel, groups, users_here, cap, width ** -0.5),
        out_shape=(
            jax.ShapeDtypeStruct((width // 64, groups * cap + 2 * STEP, 128), f32),
            jax.ShapeDtypeStruct((groups, 128), jnp.int32),
            jax.ShapeDtypeStruct(candidates.shape, bf16),
            jax.ShapeDtypeStruct(cache_keys.shape, bf16),
            jax.ShapeDtypeStruct(cache_values.shape, bf16),
        ),
        in_specs=[vmem, smem, smem] + [hbm] * 6,
        out_specs=(vmem,) * 5,
        scratch_shapes=[
            pltpu.VMEM(events.shape, bf16),
            pltpu.VMEM((blocks,) + candidates.shape, bf16),
            pltpu.VMEM((2, features, width), bf16),
            pltpu.VMEM((groups, cap + TAIL, features), bf16),
            pltpu.VMEM((half, cap + TAIL, features), bf16),
            pltpu.VMEM((users_here, width, block_rows), bf16),
            pltpu.VMEM((width, width), bf16),
            pltpu.VMEM((2, users_here, width, quarter), f32),
            pltpu.VMEM((4, users_here, 8, quarter), f32),
            pltpu.VMEM((2, users_here, width, quarter), bf16),
            pltpu.VMEM((2, users_here, width, quarter), bf16),
            pltpu.VMEM((2, users_here, 8, quarter), f32),
            pltpu.VMEM((users_here, width, quarter), bf16),
            pltpu.VMEM((users_here, 8, quarter), f32),
            pltpu.VMEM((users_here, width, quarter), bf16),
            pltpu.VMEM((users_here, 8, quarter), f32),
            dma((7,)), dma((half,)), dma((half,)), dma((half,)), dma((half,)),
            dma((3, users_here)), dma((3, users_here)),
            dma((2, 2 * users_here)), dma((2, 2 * users_here)),
            dma((2, users_here)), dma((2, users_here)),
        ],
        compiler_params=pltpu.CompilerParams(
            collective_id=0, has_side_effects=True, vmem_limit_bytes=28 * 2**20
        ),
        name="merged",
    )(
        *[
            pltpu.with_memory_space_constraint(x, pltpu.HBM)
            for x in (
                owners.reshape(1, per_event), hist_len, active, events, candidates,
                cache_keys, cache_values, w_key, w_value,
            )
        ]
    )

    return pl.pallas_call(
        functools.partial(place_kernel, groups, cap),
        out_shape=(
            jax.ShapeDtypeStruct(cache_keys.shape, bf16),
            jax.ShapeDtypeStruct(cache_values.shape, bf16),
            jax.ShapeDtypeStruct(candidates.shape, bf16),
        ),
        in_specs=[smem, smem] + [vmem] * 4,
        out_specs=(hbm,) * 3,
        scratch_shapes=[
            pltpu.VMEM((users_here, 2, block_rows, width), bf16),
            dma((users_here, 2)), dma,
        ],
        compiler_params=pltpu.CompilerParams(vmem_limit_bytes=28 * 2**20),
        name="place",
    )(counts, hist_len, made, keys, values, attended)


def solution(mesh):
    placed = (
        P("user", None),
        P("user"),
        P("user"),
        P(),
        P(),
        P("user", "pos", None),
        P("user", "pos", None),
        P("user"),
        P("user"),
        P("user", "pos", None),
    )
    return jax.shard_map(
        on_device,
        mesh=mesh,
        in_specs=placed,
        out_specs=(P("user", "pos", None), P("user", "pos", None), P("user", "pos", None)),
        check_vma=False,
    )
```

profile of v0, /device:TPU:0, one launch (start us, length us, event | category | flops | bytes accessed | tf_op | source)
XLA Modules:
  0.0 28.6 jit_solution(14731242288671329241)
XLA Ops:
  0.6 0.0 copy-start
  0.6 25.5 %merged.1 = (f32[4,2176,128]{2,1,0:T(8,128)S(1)}, s32[8,128]{1,0:T(8,128)S(1)}, bf16[2,256,256]{2,1,0:T(8,128)(2,1)S(1)}, bf16[2,1536,256]{2,1,0:T(8,128)(2,1)S(1)}, bf16[2,1536,256]{2,1,0:T(8,128)(2,1)S(1)}) custom-call(s32[1,1024]{1,0:T(1,128)} %bitcast.1, s32[2]{0:T(128)} %hist_ref.3, s32[2]{0:T(128)} %active_ref.1, bf16[1024,256]{1,0:T(8,128)(2,1)} %events_hbm.1, ...), custom_call_target="tpu_custom_call" | custom-call | tf_op jit(solution)/shard_map/merged/pallas_call | solution.py:456
  26.2 0.0 copy-done
  26.2 2.4 %place.1 = (bf16[2,1536,256]{2,1,0:T(8,128)(2,1)}, bf16[2,1536,256]{2,1,0:T(8,128)(2,1)}, bf16[2,256,256]{2,1,0:T(8,128)(2,1)}) custom-call(s32[8,128]{1,0:T(8,128)S(1)} %get-tuple-element.8.count_ref, s32[2]{0:T(128)S(1)} %copy-done, f32[4,2176,128]{2,1,0:T(8,128)S(1)} %get-tuple-element.9.made_ref, bf16[2,1536,256]{2,1,0:T(8,128)(2,1)S(1)} %get-tuple-element.10.keys_ref, ...), custom_call_target="tpu_custom_call" | custom-call | tf_op jit(solution)/shard_map/place/pallas_call | solution.py:503
Async XLA Ops:
  0.6 25.5 %copy-start = (s32[2]{0:T(128)S(1)}, s32[2]{0:T(128)}, u32[]{:S(2)}) copy-start(s32[2]{0:T(128)} %hist_ref.3) | copy-start | bytes 28
where the time goes:
time: 28.9 us; the launch traced here: 28.6 us
  Pallas kernels  27.9 us (97%)
  between operations  0.66 us (2%)
    pallas_call x1, Pallas kernels, on_device(): pl.pallas_call(functools.partial(merged_kernel, groups, users_here, cap,...  25.5 us
    pallas_call x1, Pallas kernels, on_device(): pl.pallas_call(functools.partial(place_kernel, groups, cap), out_shape=(j...  2.41 us

commit v1 on v0

--- a/solution.py
+++ b/solution.py
@@ -23,10 +23,10 @@
 
 def merged_kernel(
     groups, users_here, cap, scale,
-    owners_ref, hist_ref, active_ref, events_hbm, cand_hbm, keys_hbm, values_hbm,
+    owners_hbm, hist_hbm, active_hbm, events_hbm, cand_hbm, keys_hbm, values_hbm,
     w_key_hbm, w_value_hbm,
     fresh_ref, counts_ref, out_ref, keys_ref, values_ref,
-    events_ref, queries, weight_ref, rows_ref, packed, flipped, eye,
+    owners_ref, hist_ref, active_ref, events_ref, queries, weight_ref, rows_ref, packed, flipped, eye, turned_weight,
     acc, stat, near_out, near_part, near_stat, far_out, far_stat_out, far_part, far_stat,
     load_sem, a2a_send, a2a_recv, hop_send, hop_recv, q_send, q_recv,
     near_send, near_recv, far_send, far_recv,
@@ -47,7 +47,7 @@
 
     peers = [partner(k, low) for k in range(half)]
     near_sources = [partner(k, 1 - low) for k in range(half)]
-    sends = list(range(half))[::-1]
+    soon, mid, late = range(half // 2), range(half // 2, 3 * half // 4), range(3 * half // 4, half)
     block_rows, width = keys_ref.shape[1:]
     quarter = queries.shape[2]
 
@@ -56,11 +56,13 @@
         copy.start()
         return copy
 
+    owners_in = load(owners_hbm, owners_ref, 7)
     events_in = load(events_hbm, events_ref, 0)
     own_q = load(cand_hbm, queries.at[p], 1)
     keys_in = load(keys_hbm, keys_ref, 2)
     values_in = load(values_hbm, values_ref, 3)
     weights_in = [load(w_key_hbm, weight_ref.at[0], 4), load(w_value_hbm, weight_ref.at[1], 5)]
+    scalars_in = [load(hist_hbm, hist_ref, 8), load(active_hbm, active_ref, 9)]
 
     barrier = pltpu.get_barrier_semaphore()
     for peer in (near, far):
@@ -70,6 +72,7 @@
         def _():
             pl.semaphore_signal(barrier, inc=1, device_id={"user": peer}, device_id_type=MESH)
 
+    owners_in.wait()
     per_event = events_ref.shape[0]
     features = events_ref.shape[1]
     users = groups * users_here
@@ -109,10 +112,12 @@
     def own(k):
         return pltpu.make_async_copy(packed.at[k], rows_ref.at[me], load_sem.at[6])
 
-    def pack(k):
+    def choose(k):
+        wanted = jnp.where(dest == peers[k], slot, -1)
+        return (wanted == slot_id).astype(jnp.float32).astype(jnp.bfloat16)
+
+    def pack(k, pick):
         peer = peers[k]
-        wanted = jnp.where(dest == peer, slot, -1)
-        pick = (wanted == slot_id).astype(jnp.float32).astype(jnp.bfloat16)
         packed[k, :cap, :] = jnp.dot(
             pick, events_ref[...], preferred_element_type=jnp.float32
         ).astype(jnp.bfloat16)
@@ -147,30 +152,37 @@
         block = rows_ref.at[source]
         return hop(block, block, hop_send.at[k], hop_recv.at[k], near)
 
+
     events_in.wait()
-    early = half // 2
-    for k in sends[:early]:
-        pack(k)
+    sends = list(range(half))
+    pick = choose(sends[0])
+    for n in range(len(sends) // 4):
+        pack(sends[n], pick)
+        pick = choose(sends[n + 1])
     own_q.wait()
     pl.semaphore_wait(barrier, 1 + half + low)
     for u in range(users_here):
         q_hop(0, p, u, far).start()
     for u in range(users_here):
         q_hop(1, p, u, near).start()
-    for k in sends[:early]:
+    for k in sends[: half // 4]:
         post(k)
-    for k in sends[early:]:
-        pack(k)
-        post(k)
+    for n in range(half // 4, half):
+        after = choose(sends[n + 1]) if n + 1 < half else None
+        pack(sends[n], pick)
+        pick = after
+        post(sends[n])
 
     eye[...] = (
         lax.broadcasted_iota(jnp.int32, (width, width), 0)
         == lax.broadcasted_iota(jnp.int32, (width, width), 1)
     ).astype(jnp.float32).astype(jnp.bfloat16)
     factor = scale * math.log2(math.e)
-    position = lax.broadcasted_iota(jnp.int32, (block_rows, quarter), 0) + p * block_rows
+    position = lax.broadcasted_iota(jnp.int32, (block_rows, quarter), 0)
     keys_in.wait()
     values_in.wait()
+    for copy in scalars_in:
+        copy.wait()
 
     def flip(rows):
         return lax.dot_general(
@@ -179,6 +191,9 @@
 
     for u in range(users_here):
         flipped[u] = flip(values_ref[u])
+    for copy in weights_in:
+        copy.wait()
+    turned_weight[...] = flip(weight_ref[1])
 
     def two_rows(top, total):
         return jnp.concatenate(
@@ -240,9 +255,13 @@
             q_hop(2, far, u, near).start()
         if kind == 3:
             q_hop(2, cross, u, near).wait_recv()
+            for k in soon[u * len(soon) // users_here : (u + 1) * len(soon) // users_here]:
+                arrive(k)
 
     def finish(kind, u, scores):
-        top, total, weights = weigh(jnp.where(position < hist_ref[u], scores, -1e33), -1e29)
+        top, total, weights = weigh(
+            jnp.where(position < hist_ref[u] - p * block_rows, scores, -1e33), -1e29
+        )
         part = jnp.dot(flipped[u], weights, preferred_element_type=jnp.float32)
         stat[kind, u] = two_rows(top, total)
         if kind < 2:
@@ -256,7 +275,8 @@
 
     items = [(0, u) for u in range(users_here)]
     for u in range(users_here):
-        items += [(2, u), (1, u), (3, u)]
+        items += [(2, u)] * (u < users_here - 1) + [(1, u), (3, u)]
+    items.append((2, users_here - 1))
     last = None
     for kind, u in items:
         ready(kind, u)
@@ -266,20 +286,6 @@
         if last is not None:
             finish(*last)
         last = (kind, u, scores)
-    finish(*last)
-    send_far(users_here - 1)
-    for u in range(users_here):
-        for copy in near_copies(0, u):
-            copy.wait_recv()
-        old = stat[0, u]
-        top, total, part = merge(
-            old[0:1], old[4:5], acc[0, u], near_stat[0, u], near_part[0, u]
-        )
-        acc[0, u] = part
-        stat[0, u] = two_rows(top, total)
-    for copy in weights_in:
-        copy.wait()
-
     slots = lax.broadcasted_iota(jnp.int32, (cap, quarter), 0).astype(jnp.float32)
 
     def project(source):
@@ -301,39 +307,72 @@
             end = begin + tail[0:1, u : u + 1]
             mask.append((slots >= begin) & (slots < end))
             begin = end
-        return made[0], flip(made[1]), mask
-
-    def fresh(sources):
-        blocks = [project(source) for source in sources]
-        keys_new = jnp.concatenate([b[0] for b in blocks], axis=0)
-        flipped_new = jnp.concatenate([b[1] for b in blocks], axis=1)
-        scores = [
-            lax.dot_general(keys_new, queries[p, u], NT, preferred_element_type=jnp.float32)
-            for u in range(users_here)
+        turned = lax.dot_general(
+            turned_weight[...], raw, NT, preferred_element_type=jnp.float32
+        ).astype(jnp.bfloat16)
+        return made[0], turned, mask
+
+    def gather(sources, before=()):
+        blocks = list(before) + [project(source) for source in sources]
+        masks = [
+            jnp.concatenate([b[2][u] for b in blocks], axis=0) for u in range(users_here)
         ]
+        return (
+            jnp.concatenate([b[0] for b in blocks], axis=0),
+            jnp.concatenate([b[1] for b in blocks], axis=1),
+            masks,
+        )
+
+    def score(u, new):
+        return lax.dot_general(new[0], queries[p, u], NT, preferred_element_type=jnp.float32)
+
+    def attend(u, new, scores):
+        old = stat[0, u]
+        top, total, weights = weigh(jnp.where(new[2][u], scores, -1e33), old[0:1])
+        shrink = jnp.exp2(old[0:1] - top)
+        acc[0, u] = acc[0, u] * shrink + jnp.dot(
+            new[1], weights, preferred_element_type=jnp.float32
+        )
+        stat[0, u] = two_rows(top, total + old[4:5] * shrink)
+
+    def attend_all(new):
+        scores = [score(u, new) for u in range(users_here)]
         for u in range(users_here):
-            mask = jnp.concatenate([b[2][u] for b in blocks], axis=0)
-            old = stat[0, u]
-            top, total, weights = weigh(jnp.where(mask, scores[u], -1e33), old[0:1])
-            shrink = jnp.exp2(old[0:1] - top)
-            acc[0, u] = acc[0, u] * shrink + jnp.dot(
-                flipped_new, weights, preferred_element_type=jnp.float32
-            )
-            stat[0, u] = two_rows(top, total + old[4:5] * shrink)
-
-    soon = range(half // 2)
-    late = range(half // 2, half)
-    for k in soon:
-        arrive(k)
+            attend(u, new, scores[u])
+
     for k in soon:
         forward(k, near_sources[k]).wait_recv()
-    fresh([source for k in soon for source in (peers[k], near_sources[k])])
+    new = gather([source for k in soon for source in (peers[k], near_sources[k])])
+    finish(*last)
+    send_far(users_here - 1)
+    scores = score(0, new)
+    for u in range(users_here):
+        after = score(u + 1, new) if u + 1 < users_here else None
+        attend(u, new, scores)
+        scores = after
+        if u == 0:
+            for k in mid:
+                arrive(k)
+            mine = [project(peers[k]) for k in mid]
+    for u in range(users_here):
+        for copy in near_copies(0, u):
+            copy.wait_recv()
+    for u in range(users_here):
+        old = stat[0, u]
+        top, total, part = merge(
+            old[0:1], old[4:5], acc[0, u], near_stat[0, u], near_part[0, u]
+        )
+        acc[0, u] = part
+        stat[0, u] = two_rows(top, total)
+    for k in mid:
+        forward(k, near_sources[k]).wait_recv()
+    attend_all(gather([near_sources[k] for k in mid], mine))
     for k in late:
         arrive(k)
-    fresh([peers[k] for k in late])
+    attend_all(gather([peers[k] for k in late]))
     for k in late:
         forward(k, near_sources[k]).wait_recv()
-    fresh([near_sources[k] for k in late])
+    attend_all(gather([near_sources[k] for k in late]))
     for g in range(groups):
         counts_ref[g : g + 1, :] = rows_ref[g, cap : cap + TAIL, :128].astype(jnp.float32)[
             0:1
@@ -462,9 +501,12 @@
             jax.ShapeDtypeStruct(cache_keys.shape, bf16),
             jax.ShapeDtypeStruct(cache_values.shape, bf16),
         ),
-        in_specs=[vmem, smem, smem] + [hbm] * 6,
+        in_specs=[hbm] * 9,
         out_specs=(vmem,) * 5,
         scratch_shapes=[
+            pltpu.VMEM((1, per_event), jnp.int32),
+            pltpu.SMEM(hist_len.shape, jnp.int32),
+            pltpu.SMEM(active.shape, jnp.int32),
             pltpu.VMEM(events.shape, bf16),
             pltpu.VMEM((blocks,) + candidates.shape, bf16),
             pltpu.VMEM((2, features, width), bf16),
@@ -472,6 +514,7 @@
             pltpu.VMEM((half, cap + TAIL, features), bf16),
             pltpu.VMEM((users_here, width, block_rows), bf16),
             pltpu.VMEM((width, width), bf16),
+            pltpu.VMEM((width, features), bf16),
             pltpu.VMEM((2, users_here, width, quarter), f32),
             pltpu.VMEM((4, users_here, 8, quarter), f32),
             pltpu.VMEM((2, users_here, width, quarter), bf16),
@@ -481,7 +524,7 @@
             pltpu.VMEM((users_here, 8, quarter), f32),
             pltpu.VMEM((users_here, width, quarter), bf16),
             pltpu.VMEM((users_here, 8, quarter), f32),
-            dma((7,)), dma((half,)), dma((half,)), dma((half,)), dma((half,)),
+            dma((10,)), dma((half,)), dma((half,)), dma((half,)), dma((half,)),
             dma((3, users_here)), dma((3, users_here)),
             dma((2, 2 * users_here)), dma((2, 2 * users_here)),
             dma((2, users_here)), dma((2, users_here)),

time: 28.9 us -> 27.2 us (0.941)
  Pallas kernels: 27.9 us -> 26.3 us
    pallas_call x1, Pallas kernels: 25.5 us -> 23.9 us  [on_device(): pl.pallas_call(functools.partial(merged_kernel, groups, users_here, cap,...]
where the time goes in v1:
time: 27.2 us; the launch traced here: 27 us
  Pallas kernels  26.3 us (97%)
  between operations  0.66 us (2%)
    pallas_call x1, Pallas kernels, on_device(): pl.pallas_call(functools.partial(merged_kernel, groups, users_here, cap,...  23.9 us
    pallas_call x1, Pallas kernels, on_device(): pl.pallas_call(functools.partial(place_kernel, groups, cap), out_shape=(j...  2.41 us

profile of v1, /device:TPU:0, one launch (start us, length us, event | category | flops | bytes accessed | tf_op | source)
XLA Modules:
  0.0 27.0 jit_solution(4389883850211629591)
XLA Ops:
  0.6 0.0 copy-start
  0.6 23.9 %merged.1 = (f32[4,2176,128]{2,1,0:T(8,128)S(1)}, s32[8,128]{1,0:T(8,128)S(1)}, bf16[2,256,256]{2,1,0:T(8,128)(2,1)S(1)}, bf16[2,1536,256]{2,1,0:T(8,128)(2,1)S(1)}, bf16[2,1536,256]{2,1,0:T(8,128)(2,1)S(1)}) custom-call(s32[1,1024]{1,0:T(1,128)} %bitcast.1, s32[2]{0:T(128)} %hist_ref.1, s32[2]{0:T(128)} %active_hbm.1, bf16[1024,256]{1,0:T(8,128)(2,1)} %events_hbm.1, ...), custom_call_target="tpu_custom_call" | custom-call | tf_op jit(solution)/shard_map/merged/pallas_call | solution.py:495
  24.6 0.0 copy-done
  24.6 2.4 %place.1 = (bf16[2,1536,256]{2,1,0:T(8,128)(2,1)}, bf16[2,1536,256]{2,1,0:T(8,128)(2,1)}, bf16[2,256,256]{2,1,0:T(8,128)(2,1)}) custom-call(s32[8,128]{1,0:T(8,128)S(1)} %get-tuple-element.8.count_ref, s32[2]{0:T(128)S(1)} %copy-done, f32[4,2176,128]{2,1,0:T(8,128)S(1)} %get-tuple-element.9.made_ref, bf16[2,1536,256]{2,1,0:T(8,128)(2,1)S(1)} %get-tuple-element.10.keys_ref, ...), custom_call_target="tpu_custom_call" | custom-call | tf_op jit(solution)/shard_map/place/pallas_call | solution.py:546
Async XLA Ops:
  0.6 24.0 %copy-start = (s32[2]{0:T(128)S(1)}, s32[2]{0:T(128)}, u32[]{:S(2)}) copy-start(s32[2]{0:T(128)} %hist_ref.1) | copy-start | bytes 28

commit v2 on v1

--- a/solution.py
+++ b/solution.py
@@ -344,13 +344,13 @@
         forward(k, near_sources[k]).wait_recv()
     new = gather([source for k in soon for source in (peers[k], near_sources[k])])
     finish(*last)
-    send_far(users_here - 1)
     scores = score(0, new)
     for u in range(users_here):
         after = score(u + 1, new) if u + 1 < users_here else None
         attend(u, new, scores)
         scores = after
         if u == 0:
+            send_far(users_here - 1)
             for k in mid:
                 arrive(k)
             mine = [project(peers[k]) for k in mid]

time: 27.2 us -> 27.2 us (level)
  no operation moved by 1% of the time
where the time goes in v2:
time: 27.2 us; the launch traced here: 27 us
  Pallas kernels  26.3 us (97%)
  between operations  0.66 us (2%)
    pallas_call x1, Pallas kernels, on_device(): pl.pallas_call(functools.partial(merged_kernel, groups, users_here, cap,...  23.9 us
    pallas_call x1, Pallas kernels, on_device(): pl.pallas_call(functools.partial(place_kernel, groups, cap), out_shape=(j...  2.41 us

profile of v2, /device:TPU:0, one launch (start us, length us, event | category | flops | bytes accessed | tf_op | source)
XLA Modules:
  0.0 27.0 jit_solution(11622015736156669259)
XLA Ops:
  0.6 0.0 copy-start
  0.6 23.9 %merged.1 = (f32[4,2176,128]{2,1,0:T(8,128)S(1)}, s32[8,128]{1,0:T(8,128)S(1)}, bf16[2,256,256]{2,1,0:T(8,128)(2,1)S(1)}, bf16[2,1536,256]{2,1,0:T(8,128)(2,1)S(1)}, bf16[2,1536,256]{2,1,0:T(8,128)(2,1)S(1)}) custom-call(s32[1,1024]{1,0:T(1,128)} %bitcast.1, s32[2]{0:T(128)} %hist_ref.1, s32[2]{0:T(128)} %active_hbm.1, bf16[1024,256]{1,0:T(8,128)(2,1)} %events_hbm.1, ...), custom_call_target="tpu_custom_call" | custom-call | tf_op jit(solution)/shard_map/merged/pallas_call | solution.py:495
  24.6 0.0 copy-done
  24.6 2.4 %place.1 = (bf16[2,1536,256]{2,1,0:T(8,128)(2,1)}, bf16[2,1536,256]{2,1,0:T(8,128)(2,1)}, bf16[2,256,256]{2,1,0:T(8,128)(2,1)}) custom-call(s32[8,128]{1,0:T(8,128)S(1)} %get-tuple-element.8.count_ref, s32[2]{0:T(128)S(1)} %copy-done, f32[4,2176,128]{2,1,0:T(8,128)S(1)} %get-tuple-element.9.made_ref, bf16[2,1536,256]{2,1,0:T(8,128)(2,1)S(1)} %get-tuple-element.10.keys_ref, ...), custom_call_target="tpu_custom_call" | custom-call | tf_op jit(solution)/shard_map/place/pallas_call | solution.py:546
Async XLA Ops:
  0.6 24.0 %copy-start = (s32[2]{0:T(128)S(1)}, s32[2]{0:T(128)}, u32[]{:S(2)}) copy-start(s32[2]{0:T(128)} %hist_ref.1) | copy-start | bytes 28
